TPU v7x, 32 devices: a whole 2x2x4 slice. The times are simulated.
32 devices in a mesh: gx: 8 (over z, x), gy: 4 (over y, core).
Axes of the slice: x: 2, y: 2, z: 4, core: 2. Of those that a mesh axis runs over, the one named last changes fastest.
Arguments:
- source_tiles: bfloat16 [96, 32, 192, 384], P(('gx', 'gy')), may hold values from -6 to 6
- tile_offsets: int32 [2, 96], P(None, ('gx', 'gy')), may hold values from -128 to 896, as said below
- tile_shifts: int32 [96], P(('gx', 'gy')), may hold values from 0 to 63
- tile_counts: int32 [32], P(('gx', 'gy')), may hold values from 1 to 3, as said below
Outputs:
- merged_slab: float32 [32, 1024, 1024], P(None, 'gx', 'gy')
Inputs may be any that keep to these rules, and one draw needn't show every extreme that they name: `tile_offsets`: slot k belongs to the device of joined gx+gy index d = k // 3, that is gx index d // 4 and gy index d % 4. Its x offset lies from that gx index times 128 minus 64 up to that gx index times 128; its y offset from the gy index times 256 minus 128 up to the gy index times 256. So every tile covers its owner's whole block. `tile_counts`: entry d counts the used slots of device d; they are its first slots, the others are ignored. Both 1 and 3 occur in every draw.
All inputs are finite; a program needn't handle non-finite values.
Results may differ from a plain program's by a relative error of at most 0.0003.
Values sent between devices are 32-bit elements; how exact they have to be, the bound alone decides.
No kernel may reach another device: no remote copies, remote signals or barrier semaphores. Data moves between devices by JAX's collectives and lax.ppermute only.
A program may use at most 192 MiB of HBM per device.

v0:
```python
import functools

import jax
import jax.numpy as jnp
from jax import lax
from jax.experimental import pallas as pl
from jax.experimental.pallas import tpu as pltpu
from jax.sharding import PartitionSpec as P


BX = 128
BY = 256
RAMP = 32
CHUNKS = 4
ZB = 4


def passed_along(array, axis, by):
    count = lax.axis_size(axis)
    pairs = [(i, i + by) for i in range(count) if 0 <= i + by < count]
    return lax.ppermute(array, axis, pairs)


def ramp_of(places, length):
    rise = jnp.minimum(jnp.minimum(places + 1, length - places), RAMP).astype(jnp.float32)
    return jnp.where((places >= 0) & (places < length), rise, 0.0)


def merge_kernel(params, src, nxt, *rest, cap, tx, ty, rx, ry):
    low, mid, high, my, mx, acc, stack = rest[-7:]
    wide_x = BX + 2 * rx
    wide_y = BY + 2 * ry
    zb = src.shape[1]

    @pl.when(pl.program_id(0) == 0)
    def build():
        for k in range(cap):
            frac = (params[2 * cap + k] % 4).astype(jnp.float32) * 0.25
            place = lax.broadcasted_iota(jnp.int32, (1, wide_y), 1) - params[cap + k]
            ramp = ramp_of(place, ty)
            cell = lax.broadcasted_iota(jnp.int32, (ty, wide_y), 0)
            near = jnp.where(cell == place, ramp * (1.0 - frac), 0.0)
            far = jnp.where(cell == jnp.minimum(place + 1, ty - 1), ramp * frac, 0.0)
            my[k] = (near + far).astype(jnp.bfloat16)
        column = lax.broadcasted_iota(jnp.int32, (1, cap * tx), 1)
        start = jnp.zeros_like(column)
        frac = jnp.zeros(column.shape, jnp.float32)
        active = jnp.zeros(column.shape, jnp.float32)
        cell = column
        for k in range(cap):
            here = (column >= k * tx) & (column < (k + 1) * tx)
            start = jnp.where(here, params[k], start)
            code = params[2 * cap + k] // 4 % 4
            frac = jnp.where(here, code.astype(jnp.float32) * 0.25, frac)
            active = jnp.where(here, params[3 * cap + k].astype(jnp.float32), active)
            cell = jnp.where(here, column - k * tx, cell)
        place = lax.broadcasted_iota(jnp.int32, (wide_x, cap * tx), 0) - start
        ramp = ramp_of(place, tx) * active
        near = jnp.where(cell == place, ramp * (1.0 - frac), 0.0)
        far = jnp.where(cell == jnp.minimum(place + 1, tx - 1), ramp * frac, 0.0)
        both = (near + far).astype(jnp.bfloat16)
        mx[...] = jnp.concatenate([both, both], axis=1)
        for k in range(cap):
            acc[k, zb * tx :] = jnp.dot(nxt[k, 0], my[k], preferred_element_type=jnp.float32)

    for k in range(cap):
        rows = src[k].reshape(zb * tx, ty)
        half = wide_y // 2
        skip = half - ry
        acc[k, : zb * tx, :half] = jnp.dot(
            rows, my[k, :, :half], preferred_element_type=jnp.float32
        )
        acc[k, : zb * tx, half:] = jnp.dot(
            rows[:, skip:], my[k, skip:, half:], preferred_element_type=jnp.float32
        )
    for j in range(zb):
        for k in range(cap):
            frac = (params[2 * cap + k] // 16 % 4).astype(jnp.float32) * 0.25
            here = acc[k, j * tx : (j + 1) * tx]
            after = acc[k, (j + 1) * tx : (j + 2) * tx]
            value = (1.0 - frac) * here + frac * after
            head = value.astype(jnp.bfloat16)
            stack[j % 2, k * tx : (k + 1) * tx] = head
            tail = (value - head.astype(jnp.float32)).astype(jnp.bfloat16)
            stack[j % 2, (cap + k) * tx : (cap + k + 1) * tx] = tail
        total = jnp.dot(mx[...], stack[j % 2], preferred_element_type=jnp.float32)
        low[j] = total[:, :ry]
        mid[j] = total[:, ry : ry + BY]
        high[j] = total[:, ry + BY :]
    for k in range(cap):
        acc[k, zb * tx :] = acc[k, :tx]


def merge_chunk(source, params, first, depth, rx, ry, behind):
    cap, nz, tx, ty = source.shape
    steps = depth // ZB
    wide_x = BX + 2 * rx
    wide_y = BY + 2 * ry
    top = first // ZB + steps - 1
    after = min(first + depth, nz - 1)
    kernel = functools.partial(merge_kernel, cap=cap, tx=tx, ty=ty, rx=rx, ry=ry)
    return pl.pallas_call(
        kernel,
        grid=(steps,),
        in_specs=[
            pl.BlockSpec(memory_space=pltpu.SMEM),
            pl.BlockSpec((cap, ZB, tx, ty), lambda i: (0, top - i, 0, 0)),
            pl.BlockSpec((cap, 1, tx, ty), lambda i: (0, after, 0, 0)),
        ]
        + [pl.BlockSpec(memory_space=pl.ANY)] * len(behind),
        out_specs=[
            pl.BlockSpec((ZB, wide_x, ry), lambda i: (steps - 1 - i, 0, 0)),
            pl.BlockSpec((ZB, wide_x, BY), lambda i: (steps - 1 - i, 0, 0)),
            pl.BlockSpec((ZB, wide_x, ry), lambda i: (steps - 1 - i, 0, 0)),
        ],
        out_shape=[
            jax.ShapeDtypeStruct((depth, wide_x, ry), jnp.float32),
            jax.ShapeDtypeStruct((depth, wide_x, BY), jnp.float32),
            jax.ShapeDtypeStruct((depth, wide_x, ry), jnp.float32),
        ],
        scratch_shapes=[
            pltpu.VMEM((cap, ty, wide_y), jnp.bfloat16),
            pltpu.VMEM((wide_x, 2 * cap * tx), jnp.bfloat16),
            pltpu.VMEM((cap, (ZB + 1) * tx, wide_y), jnp.float32),
            pltpu.VMEM((2, 2 * cap * tx, wide_y), jnp.bfloat16),
        ],
        compiler_params=pltpu.CompilerParams(
            dimension_semantics=("arbitrary",), vmem_limit_bytes=48 * 1024 * 1024
        ),
        cost_estimate=pl.CostEstimate(
            flops=depth * 2 * cap * tx * wide_y * (ty + 2 * wide_x),
            bytes_accessed=depth * (cap * tx * ty * 2 + wide_x * wide_y * 4),
            transcendentals=0,
        ),
        name="merge_tiles",
    )(params, source, source, *behind)


def rows_kernel(mid, before, after, low, high, *, rx, ry):
    edge = rx + BX
    low[:, :, :ry] = mid[:, :rx, :ry] + before[:, :rx]
    low[:, :, ry:] = mid[:, :rx, ry:] + after[:, :rx]
    high[:, :, :ry] = mid[:, edge:, :ry] + before[:, edge:]
    high[:, :, ry:] = mid[:, edge:, ry:] + after[:, edge:]


def edge_rows(mid, before, after, rx, ry):
    depth = mid.shape[0]
    step = min(depth, 4)
    whole = lambda a: pl.BlockSpec((step,) + a.shape[1:], lambda i: (i, 0, 0))
    shape = jax.ShapeDtypeStruct((depth, rx, BY), jnp.float32)
    return pl.pallas_call(
        functools.partial(rows_kernel, rx=rx, ry=ry),
        grid=(depth // step,),
        in_specs=[whole(mid), whole(before), whole(after)],
        out_specs=[whole(shape), whole(shape)],
        out_shape=[shape, shape],
        compiler_params=pltpu.CompilerParams(vmem_limit_bytes=48 * 1024 * 1024),
        cost_estimate=pl.CostEstimate(
            flops=depth * 2 * rx * BY, bytes_accessed=mid.size * 8, transcendentals=0
        ),
        name="edge_rows",
    )(mid, before, after)


def finish_kernel(mid, before, after, left, right, scale, *rest, rx, ry):
    out = rest[-1]
    low = slice(rx, 2 * rx)
    high = slice(2 * rx, 3 * rx)
    for rows, place, other in ((low, slice(0, rx), left), (high, slice(rx, 2 * rx), right)):
        part = mid[:, rows, :ry] + before[:, rows] + other[:, :, :ry]
        out[:, place, :ry] = part * scale[place, :ry]
        part = mid[:, rows, ry:] + after[:, rows] + other[:, :, ry:]
        out[:, place, ry:] = part * scale[place, ry:]


def finish_chunk(pieces, scale, out, first, nz, rx, ry):
    depth = pieces[0].shape[0]
    step = min(depth, 4)
    base = first // step
    whole = lambda a: pl.BlockSpec((step,) + a.shape[1:], lambda i: (i, 0, 0))
    specs = [whole(a) for a in pieces] + [pl.BlockSpec(scale.shape, lambda i: (0, 0))]
    operands = list(pieces) + [scale]
    aliases = {}
    if out is not None:
        aliases = {len(operands): 0}
        specs.append(pl.BlockSpec(memory_space=pl.ANY))
        operands.append(out)
    return pl.pallas_call(
        functools.partial(finish_kernel, rx=rx, ry=ry),
        grid=(depth // step,),
        in_specs=specs,
        out_specs=pl.BlockSpec((step, BX, BY), lambda i: (base + i, 0, 0)),
        out_shape=jax.ShapeDtypeStruct((nz, BX, BY), jnp.float32),
        input_output_aliases=aliases,
        compiler_params=pltpu.CompilerParams(vmem_limit_bytes=48 * 1024 * 1024),
        cost_estimate=pl.CostEstimate(
            flops=depth * 4 * BX * BY, bytes_accessed=pieces[0].size * 10, transcendentals=0
        ),
        name="finish_slab",
    )(*operands)


def weight_scale(own, tx, ty):
    band = jnp.concatenate([own, passed_along(own, "gy", 1), passed_along(own, "gy", -1)], axis=0)
    from_left = passed_along(band, "gx", 1)
    from_right = passed_along(band, "gx", -1)
    near = jnp.concatenate([band, from_left, from_right], axis=0)
    cells_x = jnp.arange(BX, dtype=jnp.int32) + lax.axis_index("gx") * BX
    cells_y = jnp.arange(BY, dtype=jnp.int32) + lax.axis_index("gy") * BY
    ramp_x = ramp_of(cells_x[None] - near[:, 0:1], tx) * near[:, 2:3].astype(jnp.float32)
    ramp_y = ramp_of(cells_y[None] - near[:, 1:2], ty)
    weights = jnp.dot(ramp_x.T, ramp_y, precision=lax.Precision.HIGHEST)
    return 1.0 / jnp.maximum(weights, 1.0)


def merged(source_tiles, tile_offsets, tile_shifts, tile_counts):
    cap, nz, tx, ty = source_tiles.shape
    rx = tx - BX
    ry = ty - BY
    active = (jnp.arange(cap, dtype=jnp.int32) < tile_counts[0]).astype(jnp.int32)
    starts_x = tile_offsets[0] - lax.axis_index("gx") * BX + rx
    starts_y = tile_offsets[1] - lax.axis_index("gy") * BY + ry
    params = jnp.concatenate([starts_x, starts_y, tile_shifts, active])
    scale = weight_scale(jnp.stack([tile_offsets[0], tile_offsets[1], active], axis=1), tx, ty)
    depth = nz // CHUNKS
    out = None
    waiting = []
    edges = []
    for number in range(CHUNKS):
        first = number * depth
        behind = edges[number - 2] if number >= 2 else []
        low, mid, high = merge_chunk(source_tiles, params, first, depth, rx, ry, behind)
        after = passed_along(low, "gy", -1)
        before = passed_along(high, "gy", 1)
        edge_low, edge_high = edge_rows(mid, before, after, rx, ry)
        edges.append([edge_low])
        right = passed_along(edge_low, "gx", -1)
        left = passed_along(edge_high, "gx", 1)
        waiting.append((first, (mid, before, after, left, right)))
    for first, pieces in waiting:
        out = finish_chunk(pieces, scale, out, first, nz, rx, ry)
    return out


def solution(mesh):
    placed = (
        P(("gx", "gy"), None, None, None),
        P(None, ("gx", "gy")),
        P(("gx", "gy")),
        P(("gx", "gy")),
    )
    return jax.shard_map(
        merged, mesh=mesh, in_specs=placed, out_specs=P(None, "gx", "gy"), check_vma=False
    )
```

profile of v0, /device:TPU:20, one launch (start us, length us, event | category | flops | bytes accessed | tf_op | source)
XLA Modules:
  0.0 179.9 jit_solution(2967667176461425806)
XLA Ops:
  0.7 0.8 slice_bitcast_fusion.3
  1.4 0.7 pad_add_fusion.2.params
  2.2 8.3 %merge_tiles.6 = (f32[8,256,128]{2,1,0:T(8,128)S(1)}, f32[8,256,256]{2,1,0:T(8,128)S(1)}, f32[8,256,128]{2,1,0:T(8,128)S(1)}) custom-call(s32[12]{0:T(128)S(1)} %pad_add_fusion.2.params, bf16[3,32,192,384]{3,2,1,0:T(8,128)(2,1)} %nxt.7, bf16[3,32,192,384]{3,2,1,0:T(8,128)(2,1)} %nxt.7), custom_call_target="tpu_custom_call" | custom-call | flops 4227858432 | bytes 7733248 | tf_op jit(solution)/shard_map/merge_tiles/pallas_call | solution.py:102
  10.5 1.9 %collective-permute-start.10 = (f32[8,256,128]{2,1,0:T(8,128)S(1)}, f32[8,256,128]{2,1,0:T(8,128)S(1)}, u32[]{:S(2)}, u32[]{:S(2)}) collective-permute-start(f32[8,256,128]{2,1,0:T(8,128)S(1)} %get-tuple-element.35), channel_id=1, source_target_pairs={{0,1},{1,2},{2,3},{4,5},{5,6},{6,7},{8,9},{9,10},{10,11},{12,13},{... | collective-permute-start | bytes 3145736 | tf_op jit(solution)/shard_map/ppermute | solution.py:21
  12.4 3.6 %collective-permute-start.11 = (f32[8,256,128]{2,1,0:T(8,128)S(1)}, f32[8,256,128]{2,1,0:T(8,128)S(1)}, u32[]{:S(2)}, u32[]{:S(2)}) collective-permute-start(f32[8,256,128]{2,1,0:T(8,128)S(1)} %get-tuple-element.36), channel_id=1, source_target_pairs={{1,0},{2,1},{3,2},{5,4},{6,5},{7,6},{9,8},{10,9},{11,10},{13,12},{... | collective-permute-start | bytes 3145736 | tf_op jit(solution)/shard_map/ppermute | solution.py:21
  16.1 9.1 %merge_tiles.4 = (f32[8,256,128]{2,1,0:T(8,128)}, f32[8,256,256]{2,1,0:T(8,128)S(1)}, f32[8,256,128]{2,1,0:T(8,128)S(1)}) custom-call(s32[12]{0:T(128)S(1)} %pad_add_fusion.2.params, bf16[3,32,192,384]{3,2,1,0:T(8,128)(2,1)} %nxt.7, bf16[3,32,192,384]{3,2,1,0:T(8,128)(2,1)} %nxt.7), custom_call_target="tpu_custom_call" | custom-call | flops 4227858432 | bytes 7733248 | tf_op jit(solution)/shard_map/merge_tiles/pallas_call | solution.py:102
  25.2 1.9 %collective-permute-start = (f32[8,256,128]{2,1,0:T(8,128)S(1)}, f32[8,256,128]{2,1,0:T(8,128)S(1)}, u32[]{:S(2)}, u32[]{:S(2)}) collective-permute-start(f32[8,256,128]{2,1,0:T(8,128)S(1)} %get-tuple-element.26), channel_id=1, source_target_pairs={{0,1},{1,2},{2,3},{4,5},{5,6},{6,7},{8,9},{9,10},{10,11},{12,13},{... | collective-permute-start | bytes 3145736 | tf_op jit(solution)/shard_map/ppermute | solution.py:21
  27.1 3.6 %collective-permute-start.1 = (f32[8,256,128]{2,1,0:T(8,128)}, f32[8,256,128]{2,1,0:T(8,128)S(1)}, u32[]{:S(2)}, u32[]{:S(2)}) collective-permute-start(f32[8,256,128]{2,1,0:T(8,128)} %get-tuple-element.27), channel_id=1, source_target_pairs={{1,0},{2,1},{3,2},{5,4},{6,5},{7,6},{9,8},{10,9},{11,10},{13,12},{... | collective-permute-start | bytes 3145736 | tf_op jit(solution)/shard_map/ppermute | solution.py:21
  30.9 0.9 copy-done.6
  31.8 9.3 %merge_tiles.7 = (f32[8,256,128]{2,1,0:T(8,128)}, f32[8,256,256]{2,1,0:T(8,128)S(1)}, f32[8,256,128]{2,1,0:T(8,128)}) custom-call(s32[12]{0:T(128)S(1)} %pad_add_fusion.2.params, bf16[3,32,192,384]{3,2,1,0:T(8,128)(2,1)} %nxt.7, bf16[3,32,192,384]{3,2,1,0:T(8,128)(2,1)} %nxt.7, f32[8,64,256]{2,1,0:T(8,128)S(1)} %get-tuple-element.37.rest_0_), custom_call_target="tpu_custom_call" | custom-call | flops 4227858432 | bytes 7733248 | tf_op jit(solution)/shard_map/merge_tiles/pallas_call | solution.py:102
  41.1 1.9 %collective-permute-start.12 = (f32[8,256,128]{2,1,0:T(8,128)}, f32[8,256,128]{2,1,0:T(8,128)S(1)}, u32[]{:S(2)}, u32[]{:S(2)}) collective-permute-start(f32[8,256,128]{2,1,0:T(8,128)} %get-tuple-element.39), channel_id=1, source_target_pairs={{0,1},{1,2},{2,3},{4,5},{5,6},{6,7},{8,9},{9,10},{10,11},{12,13},{... | collective-permute-start | bytes 3145736 | tf_op jit(solution)/shard_map/ppermute | solution.py:21
  43.0 3.8 %collective-permute-start.13 = (f32[8,256,128]{2,1,0:T(8,128)}, f32[8,256,128]{2,1,0:T(8,128)S(1)}, u32[]{:S(2)}, u32[]{:S(2)}) collective-permute-start(f32[8,256,128]{2,1,0:T(8,128)} %get-tuple-element.40), channel_id=1, source_target_pairs={{1,0},{2,1},{3,2},{5,4},{6,5},{7,6},{9,8},{10,9},{11,10},{13,12},{... | collective-permute-start | bytes 3145736 | tf_op jit(solution)/shard_map/ppermute | solution.py:21
  46.9 1.1 edge_rows.4
  48.0 9.2 %merge_tiles.5 = (f32[8,256,128]{2,1,0:T(8,128)S(1)}, f32[8,256,256]{2,1,0:T(8,128)S(1)}, f32[8,256,128]{2,1,0:T(8,128)}) custom-call(s32[12]{0:T(128)S(1)} %pad_add_fusion.2.params, bf16[3,32,192,384]{3,2,1,0:T(8,128)(2,1)} %nxt.7, bf16[3,32,192,384]{3,2,1,0:T(8,128)(2,1)} %nxt.7, f32[8,64,256]{2,1,0:T(8,128)S(1)} %get-tuple-element.28.rest_0_), custom_call_target="tpu_custom_call" | custom-call | flops 4227858432 | bytes 7733248 | tf_op jit(solution)/shard_map/merge_tiles/pallas_call | solution.py:102
  57.1 1.0 copy-done.26
  58.2 1.9 %collective-permute-start.2 = (f32[8,256,128]{2,1,0:T(8,128)}, f32[8,256,128]{2,1,0:T(8,128)S(1)}, u32[]{:S(2)}, u32[]{:S(2)}) collective-permute-start(f32[8,256,128]{2,1,0:T(8,128)} %get-tuple-element.30), channel_id=1, source_target_pairs={{0,1},{1,2},{2,3},{4,5},{5,6},{6,7},{8,9},{9,10},{10,11},{12,13},{... | collective-permute-start | bytes 3145736 | tf_op jit(solution)/shard_map/ppermute | solution.py:21
  60.1 3.6 %collective-permute-start.3 = (f32[8,256,128]{2,1,0:T(8,128)}, f32[8,256,128]{2,1,0:T(8,128)S(1)}, u32[]{:S(2)}, u32[]{:S(2)}) collective-permute-start(f32[8,256,128]{2,1,0:T(8,128)} %copy-done.26), channel_id=1, source_target_pairs={{1,0},{2,1},{3,2},{5,4},{6,5},{7,6},{9,8},{10,9},{11,10},{13,12},{... | collective-permute-start | bytes 3145736 | tf_op jit(solution)/shard_map/ppermute | solution.py:21
  63.8 1.9 %collective-permute-start.6 = (s32[3,3]{0,1:T(4,128)S(1)}, s32[3,3]{0,1:T(4,128)S(1)}, u32[]{:S(2)}, u32[]{:S(2)}) collective-permute-start(s32[3,3]{0,1:T(4,128)S(1)} %pad_add_fusion), channel_id=1, source_target_pairs={{0,1},{1,2},{2,3},{4,5},{5,6},{6,7},{8,9},{9,10},{10,11},{12,13},{... | collective-permute-start | bytes 116 | tf_op jit(solution)/shard_map/ppermute | solution.py:21
  65.7 8.8 %collective-permute-done.6 = s32[3,3]{0,1:T(4,128)S(1)} collective-permute-done((s32[3,3]{0,1:T(4,128)S(1)}, s32[3,3]{0,1:T(4,128)S(1)}, u32[]{:S(2)}, u32[]{:S(2)}) %collective-permute-start.6) | collective-permute-done | bytes 68 | tf_op jit(solution)/shard_map/ppermute | solution.py:21
  74.5 1.9 %collective-permute-start.7 = (s32[3,3]{0,1:T(4,128)S(1)}, s32[3,3]{0,1:T(4,128)S(1)}, u32[]{:S(2)}, u32[]{:S(2)}) collective-permute-start(s32[3,3]{0,1:T(4,128)S(1)} %pad_add_fusion), channel_id=1, source_target_pairs={{1,0},{2,1},{3,2},{5,4},{6,5},{7,6},{9,8},{10,9},{11,10},{13,12},{... | collective-permute-start | bytes 116 | tf_op jit(solution)/shard_map/ppermute | solution.py:21
  76.4 1.3 collective-permute-done.7
  77.7 3.3 %collective-permute-start.19 = (f32[8,64,256]{2,1,0:T(8,128)S(1)}, f32[8,64,256]{2,1,0:T(8,128)S(1)}, u32[]{:S(2)}, u32[]{:S(2)}) collective-permute-start(f32[8,64,256]{2,1,0:T(8,128)S(1)} %get-tuple-element.37.rest_0_), channel_id=1, source_target_pairs={{4,0},{8,4},{12,8},{16,12},{20,16},{24,20},{28,24},{5,1},{9,5},{13... | collective-permute-start | bytes 1572872 | tf_op jit(solution)/shard_map/ppermute | solution.py:21
  81.0 2.6 %collective-permute-start.18 = (f32[8,64,256]{2,1,0:T(8,128)S(1)}, f32[8,64,256]{2,1,0:T(8,128)S(1)}, u32[]{:S(2)}, u32[]{:S(2)}) collective-permute-start(f32[8,64,256]{2,1,0:T(8,128)S(1)} %get-tuple-element.44), channel_id=1, source_target_pairs={{0,4},{4,8},{8,12},{12,16},{16,20},{20,24},{24,28},{1,5},{5,9},{9,... | collective-permute-start | bytes 1572872 | tf_op jit(solution)/shard_map/ppermute | solution.py:21
  83.6 4.2 %collective-permute-start.17 = (f32[8,64,256]{2,1,0:T(8,128)S(1)}, f32[8,64,256]{2,1,0:T(8,128)S(1)}, u32[]{:S(2)}, u32[]{:S(2)}) collective-permute-start(f32[8,64,256]{2,1,0:T(8,128)S(1)} %get-tuple-element.28.rest_0_), channel_id=1, source_target_pairs={{4,0},{8,4},{12,8},{16,12},{20,16},{24,20},{28,24},{5,1},{9,5},{13... | collective-permute-start | bytes 1572872 | tf_op jit(solution)/shard_map/ppermute | solution.py:21
  87.9 1.1 edge_rows.7
  89.0 2.0 %collective-permute-start.8 = (s32[9,3]{0,1:T(4,128)S(1)}, s32[9,3]{0,1:T(4,128)S(1)}, u32[]{:S(2)}, u32[]{:S(2)}) collective-permute-start(s32[9,3]{0,1:T(4,128)S(1)} %pad_add_fusion.1), channel_id=1, source_target_pairs={{0,4},{4,8},{8,12},{12,16},{16,20},{20,24},{24,28},{1,5},{5,9},{9,... | collective-permute-start | bytes 332 | tf_op jit(solution)/shard_map/ppermute | solution.py:21
  91.0 4.7 %collective-permute-start.9 = (s32[9,3]{0,1:T(4,128)S(1)}, s32[9,3]{0,1:T(4,128)S(1)}, u32[]{:S(2)}, u32[]{:S(2)}) collective-permute-start(s32[9,3]{0,1:T(4,128)S(1)} %pad_add_fusion.1), channel_id=1, source_target_pairs={{4,0},{8,4},{12,8},{16,12},{20,16},{24,20},{28,24},{5,1},{9,5},{13... | collective-permute-start | bytes 332 | tf_op jit(solution)/shard_map/ppermute | solution.py:21
  95.8 1.1 edge_rows.5
  96.9 19.1 %collective-permute-done.8 = s32[9,3]{0,1:T(4,128)S(1)} collective-permute-done((s32[9,3]{0,1:T(4,128)S(1)}, s32[9,3]{0,1:T(4,128)S(1)}, u32[]{:S(2)}, u32[]{:S(2)}) %collective-permute-start.8) | collective-permute-done | bytes 140 | tf_op jit(solution)/shard_map/ppermute | solution.py:21
  115.9 4.4 %collective-permute-start.16 = (f32[8,64,256]{2,1,0:T(8,128)}, f32[8,64,256]{2,1,0:T(8,128)}, u32[]{:S(2)}, u32[]{:S(2)}) collective-permute-start(f32[8,64,256]{2,1,0:T(8,128)} %get-tuple-element.43), channel_id=1, source_target_pairs={{0,4},{4,8},{8,12},{12,16},{16,20},{20,24},{24,28},{1,5},{5,9},{9,... | collective-permute-start | bytes 1572872 | tf_op jit(solution)/shard_map/ppermute | solution.py:21
  120.3 1.9 %collective-permute-start.14 = (f32[8,64,256]{2,1,0:T(8,128)}, f32[8,64,256]{2,1,0:T(8,128)}, u32[]{:S(2)}, u32[]{:S(2)}) collective-permute-start(f32[8,64,256]{2,1,0:T(8,128)} %get-tuple-element.41), channel_id=1, source_target_pairs={{0,4},{4,8},{8,12},{12,16},{16,20},{20,24},{24,28},{1,5},{5,9},{9,... | collective-permute-start | bytes 1572872 | tf_op jit(solution)/shard_map/ppermute | solution.py:21
  122.3 0.8 copy-done.20
  123.1 4.8 %collective-permute-start.15 = (f32[8,64,256]{2,1,0:T(8,128)}, f32[8,64,256]{2,1,0:T(8,128)}, u32[]{:S(2)}, u32[]{:S(2)}) collective-permute-start(f32[8,64,256]{2,1,0:T(8,128)} %get-tuple-element.42), channel_id=1, source_target_pairs={{4,0},{8,4},{12,8},{16,12},{20,16},{24,20},{28,24},{5,1},{9,5},{13... | collective-permute-start | bytes 1572872 | tf_op jit(solution)/shard_map/ppermute | solution.py:21
  127.9 0.8 copy-done.22
  128.7 1.9 %collective-permute-start.4 = (f32[8,64,256]{2,1,0:T(8,128)}, f32[8,64,256]{2,1,0:T(8,128)}, u32[]{:S(2)}, u32[]{:S(2)}) collective-permute-start(f32[8,64,256]{2,1,0:T(8,128)} %get-tuple-element.32), channel_id=1, source_target_pairs={{0,4},{4,8},{8,12},{12,16},{16,20},{20,24},{24,28},{1,5},{5,9},{9,... | collective-permute-start | bytes 1572872 | tf_op jit(solution)/shard_map/ppermute | solution.py:21
  130.6 0.8 copy-done.24
  131.4 4.8 %collective-permute-start.5 = (f32[8,64,256]{2,1,0:T(8,128)}, f32[8,64,256]{2,1,0:T(8,128)}, u32[]{:S(2)}, u32[]{:S(2)}) collective-permute-start(f32[8,64,256]{2,1,0:T(8,128)} %get-tuple-element.33), channel_id=1, source_target_pairs={{4,0},{8,4},{12,8},{16,12},{20,16},{24,20},{28,24},{5,1},{9,5},{13... | collective-permute-start | bytes 1572872 | tf_op jit(solution)/shard_map/ppermute | solution.py:21
  136.8 1.2 copy-done.7
  138.0 1.0 copy-done.21
  139.0 1.0 copy-done.23
  140.1 1.1 finish_slab.4.rest_0_
  141.2 14.2 %collective-permute-done.16.left = f32[8,64,256]{2,1,0:T(8,128)} collective-permute-done((f32[8,64,256]{2,1,0:T(8,128)}, f32[8,64,256]{2,1,0:T(8,128)}, u32[]{:S(2)}, u32[]{:S(2)}) %collective-permute-start.16) | collective-permute-done | bytes 524320 | tf_op jit(solution)/shard_map/ppermute | solution.py:21
  155.4 2.0 %finish_slab.5.rest_0_ = f32[32,128,256]{2,1,0:T(8,128)} custom-call(f32[8,256,256]{2,1,0:T(8,128)S(1)} %copy-done.1, f32[8,256,128]{2,1,0:T(8,128)S(1)} %copy-done.9, f32[8,256,128]{2,1,0:T(8,128)S(1)} %copy-done.11, f32[8,64,256]{2,1,0:T(8,128)} %collective-permute-done.16.left, f32[8,64,256]{2,1,0:T(8,128)S(1)} %copy-done.25, ...), custom_call_target="tpu_custom_call", output_to_operand_aliasing={{}: (6, {})} | custom-call | flops 1048576 | bytes 5242880 | tf_op jit(solution)/shard_map/finish_slab/pallas_call | solution.py:189
  157.4 9.2 %collective-permute-done.14.left = f32[8,64,256]{2,1,0:T(8,128)} collective-permute-done((f32[8,64,256]{2,1,0:T(8,128)}, f32[8,64,256]{2,1,0:T(8,128)}, u32[]{:S(2)}, u32[]{:S(2)}) %collective-permute-start.14) | collective-permute-done | bytes 524320 | tf_op jit(solution)/shard_map/ppermute | solution.py:21
  166.7 2.1 %finish_slab.6.rest_0_ = f32[32,128,256]{2,1,0:T(8,128)} custom-call(f32[8,256,256]{2,1,0:T(8,128)S(1)} %copy-done.3, f32[8,256,128]{2,1,0:T(8,128)S(1)} %copy-done.13, f32[8,256,128]{2,1,0:T(8,128)S(1)} %copy-done.15, f32[8,64,256]{2,1,0:T(8,128)} %collective-permute-done.14.left, ...), custom_call_target="tpu_custom_call", output_to_operand_aliasing={{}: (6, {})} | custom-call | flops 1048576 | bytes 5242880 | tf_op jit(solution)/shard_map/finish_slab/pallas_call | solution.py:189
  168.8 8.1 %collective-permute-done.4.left = f32[8,64,256]{2,1,0:T(8,128)} collective-permute-done((f32[8,64,256]{2,1,0:T(8,128)}, f32[8,64,256]{2,1,0:T(8,128)}, u32[]{:S(2)}, u32[]{:S(2)}) %collective-permute-start.4) | collective-permute-done | bytes 524320 | tf_op jit(solution)/shard_map/ppermute | solution.py:21
  176.9 0.9 collective-permute-done.5.right
  177.8 2.1 %finish_slab.7 = f32[32,128,256]{2,1,0:T(8,128)} custom-call(f32[8,256,256]{2,1,0:T(8,128)S(1)} %copy-done.5, f32[8,256,128]{2,1,0:T(8,128)S(1)} %copy-done.17, f32[8,256,128]{2,1,0:T(8,128)S(1)} %copy-done.19, f32[8,64,256]{2,1,0:T(8,128)} %collective-permute-done.4.left, ...), custom_call_target="tpu_custom_call", output_to_operand_aliasing={{}: (6, {})} | custom-call | flops 1048576 | bytes 5242880 | tf_op jit(solution)/shard_map/finish_slab/pallas_call | solution.py:189
  (69 shorter events, 0.9 us)
Async XLA Ops:
  10.5 20.3 %collective-permute-start.10 = (f32[8,256,128]{2,1,0:T(8,128)S(1)}, f32[8,256,128]{2,1,0:T(8,128)S(1)}, u32[]{:S(2)}, u32[]{:S(2)}) collective-permute-start(f32[8,256,128]{2,1,0:T(8,128)S(1)} %get-tuple-element.35), channel_id=1, source_target_pairs={{0,1},{1,2},{2,3},{4,5},{5,6},{6,7},{8,9},{9,10},{10,11},{12,13},{... | collective-permute-start | bytes 3145736 | tf_op jit(solution)/shard_map/ppermute | solution.py:21
  12.4 18.4 %collective-permute-start.11 = (f32[8,256,128]{2,1,0:T(8,128)S(1)}, f32[8,256,128]{2,1,0:T(8,128)S(1)}, u32[]{:S(2)}, u32[]{:S(2)}) collective-permute-start(f32[8,256,128]{2,1,0:T(8,128)S(1)} %get-tuple-element.36), channel_id=1, source_target_pairs={{1,0},{2,1},{3,2},{5,4},{6,5},{7,6},{9,8},{10,9},{11,10},{13,12},{... | collective-permute-start | bytes 3145736 | tf_op jit(solution)/shard_map/ppermute | solution.py:21
  25.2 21.7 %copy-start = (f32[8,256,256]{2,1,0:T(8,128)}, f32[8,256,256]{2,1,0:T(8,128)S(1)}, u32[]{:S(2)}) copy-start(f32[8,256,256]{2,1,0:T(8,128)S(1)} %get-tuple-element.25.mid) | copy-start | bytes 6291460
  25.2 21.7 %collective-permute-start = (f32[8,256,128]{2,1,0:T(8,128)S(1)}, f32[8,256,128]{2,1,0:T(8,128)S(1)}, u32[]{:S(2)}, u32[]{:S(2)}) collective-permute-start(f32[8,256,128]{2,1,0:T(8,128)S(1)} %get-tuple-element.26), channel_id=1, source_target_pairs={{0,1},{1,2},{2,3},{4,5},{5,6},{6,7},{8,9},{9,10},{10,11},{12,13},{... | collective-permute-start | bytes 3145736 | tf_op jit(solution)/shard_map/ppermute | solution.py:21
  27.1 19.8 %collective-permute-start.1 = (f32[8,256,128]{2,1,0:T(8,128)}, f32[8,256,128]{2,1,0:T(8,128)S(1)}, u32[]{:S(2)}, u32[]{:S(2)}) collective-permute-start(f32[8,256,128]{2,1,0:T(8,128)} %get-tuple-element.27), channel_id=1, source_target_pairs={{1,0},{2,1},{3,2},{5,4},{6,5},{7,6},{9,8},{10,9},{11,10},{13,12},{... | collective-permute-start | bytes 3145736 | tf_op jit(solution)/shard_map/ppermute | solution.py:21
  30.8 1.0 copy-start.6
  41.1 46.8 %copy-start.2 = (f32[8,256,256]{2,1,0:T(8,128)}, f32[8,256,256]{2,1,0:T(8,128)S(1)}, u32[]{:S(2)}) copy-start(f32[8,256,256]{2,1,0:T(8,128)S(1)} %get-tuple-element.38.mid) | copy-start | bytes 6291460
  41.1 39.9 %collective-permute-start.12 = (f32[8,256,128]{2,1,0:T(8,128)}, f32[8,256,128]{2,1,0:T(8,128)S(1)}, u32[]{:S(2)}, u32[]{:S(2)}) collective-permute-start(f32[8,256,128]{2,1,0:T(8,128)} %get-tuple-element.39), channel_id=1, source_target_pairs={{0,1},{1,2},{2,3},{4,5},{5,6},{6,7},{8,9},{9,10},{10,11},{12,13},{... | collective-permute-start | bytes 3145736 | tf_op jit(solution)/shard_map/ppermute | solution.py:21
  43.0 40.6 %collective-permute-start.13 = (f32[8,256,128]{2,1,0:T(8,128)}, f32[8,256,128]{2,1,0:T(8,128)S(1)}, u32[]{:S(2)}, u32[]{:S(2)}) collective-permute-start(f32[8,256,128]{2,1,0:T(8,128)} %get-tuple-element.40), channel_id=1, source_target_pairs={{1,0},{2,1},{3,2},{5,4},{6,5},{7,6},{9,8},{10,9},{11,10},{13,12},{... | collective-permute-start | bytes 3145736 | tf_op jit(solution)/shard_map/ppermute | solution.py:21
  46.8 10.3 %copy-start.8 = (f32[8,256,128]{2,1,0:T(8,128)}, f32[8,256,128]{2,1,0:T(8,128)S(1)}, u32[]{:S(2)}) copy-start(f32[8,256,128]{2,1,0:T(8,128)S(1)} %collective-permute-done.before) | copy-start | bytes 3145732
  46.9 10.3 %copy-start.10 = (f32[8,256,128]{2,1,0:T(8,128)}, f32[8,256,128]{2,1,0:T(8,128)S(1)}, u32[]{:S(2)}) copy-start(f32[8,256,128]{2,1,0:T(8,128)S(1)} %collective-permute-done.1.after) | copy-start | bytes 3145732
  57.1 1.1 copy-start.26
  58.2 38.7 %copy-start.4 = (f32[8,256,256]{2,1,0:T(8,128)}, f32[8,256,256]{2,1,0:T(8,128)S(1)}, u32[]{:S(2)}) copy-start(f32[8,256,256]{2,1,0:T(8,128)S(1)} %get-tuple-element.29.mid) | copy-start | bytes 6291460
  58.2 30.8 %collective-permute-start.2 = (f32[8,256,128]{2,1,0:T(8,128)}, f32[8,256,128]{2,1,0:T(8,128)S(1)}, u32[]{:S(2)}, u32[]{:S(2)}) collective-permute-start(f32[8,256,128]{2,1,0:T(8,128)} %get-tuple-element.30), channel_id=1, source_target_pairs={{0,1},{1,2},{2,3},{4,5},{5,6},{6,7},{8,9},{9,10},{10,11},{12,13},{... | collective-permute-start | bytes 3145736 | tf_op jit(solution)/shard_map/ppermute | solution.py:21
  60.1 30.9 %collective-permute-start.3 = (f32[8,256,128]{2,1,0:T(8,128)}, f32[8,256,128]{2,1,0:T(8,128)S(1)}, u32[]{:S(2)}, u32[]{:S(2)}) collective-permute-start(f32[8,256,128]{2,1,0:T(8,128)} %copy-done.26), channel_id=1, source_target_pairs={{1,0},{2,1},{3,2},{5,4},{6,5},{7,6},{9,8},{10,9},{11,10},{13,12},{... | collective-permute-start | bytes 3145736 | tf_op jit(solution)/shard_map/ppermute | solution.py:21
  63.8 10.7 %collective-permute-start.6 = (s32[3,3]{0,1:T(4,128)S(1)}, s32[3,3]{0,1:T(4,128)S(1)}, u32[]{:S(2)}, u32[]{:S(2)}) collective-permute-start(s32[3,3]{0,1:T(4,128)S(1)} %pad_add_fusion), channel_id=1, source_target_pairs={{0,1},{1,2},{2,3},{4,5},{5,6},{6,7},{8,9},{9,10},{10,11},{12,13},{... | collective-permute-start | bytes 116 | tf_op jit(solution)/shard_map/ppermute | solution.py:21
  74.5 3.2 %collective-permute-start.7 = (s32[3,3]{0,1:T(4,128)S(1)}, s32[3,3]{0,1:T(4,128)S(1)}, u32[]{:S(2)}, u32[]{:S(2)}) collective-permute-start(s32[3,3]{0,1:T(4,128)S(1)} %pad_add_fusion), channel_id=1, source_target_pairs={{1,0},{2,1},{3,2},{5,4},{6,5},{7,6},{9,8},{10,9},{11,10},{13,12},{... | collective-permute-start | bytes 116 | tf_op jit(solution)/shard_map/ppermute | solution.py:21
  77.7 44.5 %collective-permute-start.19 = (f32[8,64,256]{2,1,0:T(8,128)S(1)}, f32[8,64,256]{2,1,0:T(8,128)S(1)}, u32[]{:S(2)}, u32[]{:S(2)}) collective-permute-start(f32[8,64,256]{2,1,0:T(8,128)S(1)} %get-tuple-element.37.rest_0_), channel_id=1, source_target_pairs={{4,0},{8,4},{12,8},{16,12},{20,16},{24,20},{28,24},{5,1},{9,5},{13... | collective-permute-start | bytes 1572872 | tf_op jit(solution)/shard_map/ppermute | solution.py:21
  81.0 15.8 %copy-start.12 = (f32[8,256,128]{2,1,0:T(8,128)}, f32[8,256,128]{2,1,0:T(8,128)S(1)}, u32[]{:S(2)}) copy-start(f32[8,256,128]{2,1,0:T(8,128)S(1)} %collective-permute-done.12.before) | copy-start | bytes 3145732
  81.0 46.8 %collective-permute-start.18 = (f32[8,64,256]{2,1,0:T(8,128)S(1)}, f32[8,64,256]{2,1,0:T(8,128)S(1)}, u32[]{:S(2)}, u32[]{:S(2)}) collective-permute-start(f32[8,64,256]{2,1,0:T(8,128)S(1)} %get-tuple-element.44), channel_id=1, source_target_pairs={{0,4},{4,8},{8,12},{12,16},{16,20},{20,24},{24,28},{1,5},{5,9},{9,... | collective-permute-start | bytes 1572872 | tf_op jit(solution)/shard_map/ppermute | solution.py:21
  83.6 5.4 %copy-start.14 = (f32[8,256,128]{2,1,0:T(8,128)}, f32[8,256,128]{2,1,0:T(8,128)S(1)}, u32[]{:S(2)}) copy-start(f32[8,256,128]{2,1,0:T(8,128)S(1)} %collective-permute-done.13.after) | copy-start | bytes 3145732
  83.6 47.0 %collective-permute-start.17 = (f32[8,64,256]{2,1,0:T(8,128)S(1)}, f32[8,64,256]{2,1,0:T(8,128)S(1)}, u32[]{:S(2)}, u32[]{:S(2)}) collective-permute-start(f32[8,64,256]{2,1,0:T(8,128)S(1)} %get-tuple-element.28.rest_0_), channel_id=1, source_target_pairs={{4,0},{8,4},{12,8},{16,12},{20,16},{24,20},{28,24},{5,1},{9,5},{13... | collective-permute-start | bytes 1572872 | tf_op jit(solution)/shard_map/ppermute | solution.py:21
  89.0 27.0 %copy-start.16 = (f32[8,256,128]{2,1,0:T(8,128)}, f32[8,256,128]{2,1,0:T(8,128)S(1)}, u32[]{:S(2)}) copy-start(f32[8,256,128]{2,1,0:T(8,128)S(1)} %collective-permute-done.2.before) | copy-start | bytes 3145732
  89.0 27.0 %collective-permute-start.8 = (s32[9,3]{0,1:T(4,128)S(1)}, s32[9,3]{0,1:T(4,128)S(1)}, u32[]{:S(2)}, u32[]{:S(2)}) collective-permute-start(s32[9,3]{0,1:T(4,128)S(1)} %pad_add_fusion.1), channel_id=1, source_target_pairs={{0,4},{4,8},{8,12},{12,16},{16,20},{20,24},{24,28},{1,5},{5,9},{9,... | collective-permute-start | bytes 332 | tf_op jit(solution)/shard_map/ppermute | solution.py:21
  91.0 24.9 %copy-start.18 = (f32[8,256,128]{2,1,0:T(8,128)}, f32[8,256,128]{2,1,0:T(8,128)S(1)}, u32[]{:S(2)}) copy-start(f32[8,256,128]{2,1,0:T(8,128)S(1)} %collective-permute-done.3.after) | copy-start | bytes 3145732
  91.0 29.3 %collective-permute-start.9 = (s32[9,3]{0,1:T(4,128)S(1)}, s32[9,3]{0,1:T(4,128)S(1)}, u32[]{:S(2)}, u32[]{:S(2)}) collective-permute-start(s32[9,3]{0,1:T(4,128)S(1)} %pad_add_fusion.1), channel_id=1, source_target_pairs={{4,0},{8,4},{12,8},{16,12},{20,16},{24,20},{28,24},{5,1},{9,5},{13... | collective-permute-start | bytes 332 | tf_op jit(solution)/shard_map/ppermute | solution.py:21
  115.9 39.5 %collective-permute-start.16 = (f32[8,64,256]{2,1,0:T(8,128)}, f32[8,64,256]{2,1,0:T(8,128)}, u32[]{:S(2)}, u32[]{:S(2)}) collective-permute-start(f32[8,64,256]{2,1,0:T(8,128)} %get-tuple-element.43), channel_id=1, source_target_pairs={{0,4},{4,8},{8,12},{12,16},{16,20},{20,24},{24,28},{1,5},{5,9},{9,... | collective-permute-start | bytes 1572872 | tf_op jit(solution)/shard_map/ppermute | solution.py:21
  120.3 46.3 %collective-permute-start.14 = (f32[8,64,256]{2,1,0:T(8,128)}, f32[8,64,256]{2,1,0:T(8,128)}, u32[]{:S(2)}, u32[]{:S(2)}) collective-permute-start(f32[8,64,256]{2,1,0:T(8,128)} %get-tuple-element.41), channel_id=1, source_target_pairs={{0,4},{4,8},{8,12},{12,16},{16,20},{20,24},{24,28},{1,5},{5,9},{9,... | collective-permute-start | bytes 1572872 | tf_op jit(solution)/shard_map/ppermute | solution.py:21
  122.3 0.8 copy-start.20
  123.1 43.6 %collective-permute-start.15 = (f32[8,64,256]{2,1,0:T(8,128)}, f32[8,64,256]{2,1,0:T(8,128)}, u32[]{:S(2)}, u32[]{:S(2)}) collective-permute-start(f32[8,64,256]{2,1,0:T(8,128)} %get-tuple-element.42), channel_id=1, source_target_pairs={{4,0},{8,4},{12,8},{16,12},{20,16},{24,20},{28,24},{5,1},{9,5},{13... | collective-permute-start | bytes 1572872 | tf_op jit(solution)/shard_map/ppermute | solution.py:21
  127.9 0.8 copy-start.22
  128.7 48.2 %collective-permute-start.4 = (f32[8,64,256]{2,1,0:T(8,128)}, f32[8,64,256]{2,1,0:T(8,128)}, u32[]{:S(2)}, u32[]{:S(2)}) collective-permute-start(f32[8,64,256]{2,1,0:T(8,128)} %get-tuple-element.32), channel_id=1, source_target_pairs={{0,4},{4,8},{8,12},{12,16},{16,20},{20,24},{24,28},{1,5},{5,9},{9,... | collective-permute-start | bytes 1572872 | tf_op jit(solution)/shard_map/ppermute | solution.py:21
  130.6 0.8 copy-start.24
  131.4 46.4 %collective-permute-start.5 = (f32[8,64,256]{2,1,0:T(8,128)}, f32[8,64,256]{2,1,0:T(8,128)}, u32[]{:S(2)}, u32[]{:S(2)}) collective-permute-start(f32[8,64,256]{2,1,0:T(8,128)} %get-tuple-element.33), channel_id=1, source_target_pairs={{4,0},{8,4},{12,8},{16,12},{20,16},{24,20},{28,24},{5,1},{9,5},{13... | collective-permute-start | bytes 1572872 | tf_op jit(solution)/shard_map/ppermute | solution.py:21
  136.8 1.2 copy-start.7
  138.0 1.0 copy-start.21
  139.0 1.0 copy-start.23
  140.1 15.3 %copy-start.1 = (f32[8,256,256]{2,1,0:T(8,128)S(1)}, f32[8,256,256]{2,1,0:T(8,128)}, u32[]{:S(2)}) copy-start(f32[8,256,256]{2,1,0:T(8,128)} %copy-done) | copy-start | bytes 6291460
  140.1 15.3 %copy-start.9 = (f32[8,256,128]{2,1,0:T(8,128)S(1)}, f32[8,256,128]{2,1,0:T(8,128)}, u32[]{:S(2)}) copy-start(f32[8,256,128]{2,1,0:T(8,128)} %copy-done.8) | copy-start | bytes 3145732
  140.1 15.3 %copy-start.11 = (f32[8,256,128]{2,1,0:T(8,128)S(1)}, f32[8,256,128]{2,1,0:T(8,128)}, u32[]{:S(2)}) copy-start(f32[8,256,128]{2,1,0:T(8,128)} %copy-done.10) | copy-start | bytes 3145732
  140.1 15.3 %copy-start.25 = (f32[8,64,256]{2,1,0:T(8,128)S(1)}, f32[8,64,256]{2,1,0:T(8,128)}, u32[]{:S(2)}) copy-start(f32[8,64,256]{2,1,0:T(8,128)} %copy-done.24) | copy-start | bytes 1572868
  141.2 25.5 %copy-start.3 = (f32[8,256,256]{2,1,0:T(8,128)S(1)}, f32[8,256,256]{2,1,0:T(8,128)}, u32[]{:S(2)}) copy-start(f32[8,256,256]{2,1,0:T(8,128)} %copy-done.2) | copy-start | bytes 6291460
  141.2 25.5 %copy-start.13 = (f32[8,256,128]{2,1,0:T(8,128)S(1)}, f32[8,256,128]{2,1,0:T(8,128)}, u32[]{:S(2)}) copy-start(f32[8,256,128]{2,1,0:T(8,128)} %copy-done.12) | copy-start | bytes 3145732
  141.2 25.5 %copy-start.15 = (f32[8,256,128]{2,1,0:T(8,128)S(1)}, f32[8,256,128]{2,1,0:T(8,128)}, u32[]{:S(2)}) copy-start(f32[8,256,128]{2,1,0:T(8,128)} %copy-done.14) | copy-start | bytes 3145732
  157.4 20.4 %copy-start.5 = (f32[8,256,256]{2,1,0:T(8,128)S(1)}, f32[8,256,256]{2,1,0:T(8,128)}, u32[]{:S(2)}) copy-start(f32[8,256,256]{2,1,0:T(8,128)} %copy-done.4) | copy-start | bytes 6291460
  157.4 20.4 %copy-start.17 = (f32[8,256,128]{2,1,0:T(8,128)S(1)}, f32[8,256,128]{2,1,0:T(8,128)}, u32[]{:S(2)}) copy-start(f32[8,256,128]{2,1,0:T(8,128)} %copy-done.16) | copy-start | bytes 3145732
  157.4 20.4 %copy-start.19 = (f32[8,256,128]{2,1,0:T(8,128)S(1)}, f32[8,256,128]{2,1,0:T(8,128)}, u32[]{:S(2)}) copy-start(f32[8,256,128]{2,1,0:T(8,128)} %copy-done.18) | copy-start | bytes 3145732
where the time goes:
time: 181 us; the launch traced here: 180 us
  waiting for transfers between devices  61.7 us (34%)
  starting transfers between devices  60.8 us (34%)
  Pallas kernels  46.6 us (26%)
  local copies, waits for them, and re-layouts  7.76 us (4%)
    ppermute x20, waiting for transfers between devices, passed_along(): return lax.ppermute(array, axis, pairs)  61.7 us
    ppermute x20, starting transfers between devices, passed_along(): return lax.ppermute(array, axis, pairs)  60.8 us
    pallas_call x4, Pallas kernels, merge_chunk(): pl.pallas_call(kernel, grid=(steps,), in_specs=[pl.BlockSpec(memory_space...  35.8 us
    unnamed x54, local copies, waits for them, and re-layouts  7.66 us
    pallas_call x4, Pallas kernels, finish_chunk(): pl.pallas_call(functools.partial(finish_kernel, rx=rx, ry=ry), grid=(dept...  7.33 us
  transfers between devices with their start and end apart: 20, of which 7 were waited for; matrix products, arithmetic and copies ran while one was open for 0% of the time, Pallas kernels for 20%

commit v1 on v0

--- a/solution.py
+++ b/solution.py
@@ -12,7 +12,7 @@
 BY = 256
 RAMP = 32
 CHUNKS = 4
-ZB = 4
+ZB = 2
 
 
 def passed_along(array, axis, by):
@@ -146,7 +146,7 @@
 
 def edge_rows(mid, before, after, rx, ry):
     depth = mid.shape[0]
-    step = min(depth, 4)
+    step = 2
     whole = lambda a: pl.BlockSpec((step,) + a.shape[1:], lambda i: (i, 0, 0))
     shape = jax.ShapeDtypeStruct((depth, rx, BY), jnp.float32)
     return pl.pallas_call(
@@ -176,7 +176,7 @@
 
 def finish_chunk(pieces, scale, out, first, nz, rx, ry):
     depth = pieces[0].shape[0]
-    step = min(depth, 4)
+    step = 2
     base = first // step
     whole = lambda a: pl.BlockSpec((step,) + a.shape[1:], lambda i: (i, 0, 0))
     specs = [whole(a) for a in pieces] + [pl.BlockSpec(scale.shape, lambda i: (0, 0))]
@@ -223,12 +223,16 @@
     starts_y = tile_offsets[1] - lax.axis_index("gy") * BY + ry
     params = jnp.concatenate([starts_x, starts_y, tile_shifts, active])
     scale = weight_scale(jnp.stack([tile_offsets[0], tile_offsets[1], active], axis=1), tx, ty)
-    depth = nz // CHUNKS
+    shift = nz // (4 * CHUNKS)
+    depths = [nz // CHUNKS] * CHUNKS
+    depths[0] -= shift
+    depths[-1] += shift
     out = None
     waiting = []
     edges = []
     for number in range(CHUNKS):
-        first = number * depth
+        depth = depths[number]
+        first = sum(depths[:number])
         behind = edges[number - 2] if number >= 2 else []
         low, mid, high = merge_chunk(source_tiles, params, first, depth, rx, ry, behind)
         after = passed_along(low, "gy", -1)

time: 181 us -> 196 us (1.083)
  the two profiles are of different devices: /device:TPU:20 before, /device:TPU:0 now
where the time goes in v1:
time: 196 us; the launch traced here: 194 us
  starting transfers between devices  62.8 us (32%)
  waiting for transfers between devices  60.7 us (31%)
  Pallas kernels  58.3 us (30%)
  local copies, waits for them, and re-layouts  9.62 us (5%)
    ppermute x20, starting transfers between devices, passed_along(): return lax.ppermute(array, axis, pairs)  62.8 us
    ppermute x20, waiting for transfers between devices, passed_along(): return lax.ppermute(array, axis, pairs)  60.7 us
    pallas_call x4, Pallas kernels, merge_chunk(): pl.pallas_call(kernel, grid=(steps,), in_specs=[pl.BlockSpec(memory_space...  37.7 us
    pallas_call x4, Pallas kernels, finish_chunk(): pl.pallas_call(functools.partial(finish_kernel, rx=rx, ry=ry), grid=(dept...  12.9 us
    unnamed x50, local copies, waits for them, and re-layouts  9.52 us
    pallas_call x4, Pallas kernels, edge_rows(): pl.pallas_call(functools.partial(rows_kernel, rx=rx, ry=ry), grid=(depth...  7.67 us
  transfers between devices with their start and end apart: 20, of which 8 were waited for; matrix products, arithmetic and copies ran while one was open for 0% of the time, Pallas kernels for 23%

profile of v1, /device:TPU:0, one launch (start us, length us, event | category | flops | bytes accessed | tf_op | source)
XLA Modules:
  0.0 194.5 jit_solution(18277568104080322711)
XLA Ops:
  0.7 0.8 slice_bitcast_fusion.3
  2.2 8.8 %merge_tiles.4 = (f32[8,256,128]{2,1,0:T(8,128)S(1)}, f32[8,256,256]{2,1,0:T(8,128)S(1)}, f32[8,256,128]{2,1,0:T(8,128)S(1)}) custom-call(s32[12]{0:T(128)S(1)} %pad_add_fusion.2.params, bf16[3,32,192,384]{3,2,1,0:T(8,128)(2,1)} %nxt.7, bf16[3,32,192,384]{3,2,1,0:T(8,128)(2,1)} %nxt.7), custom_call_target="tpu_custom_call" | custom-call | flops 4227858432 | bytes 7733248 | tf_op jit(solution)/shard_map/merge_tiles/pallas_call | solution.py:102
  10.9 2.5 %collective-permute-start = (f32[8,256,128]{2,1,0:T(8,128)S(1)}, f32[8,256,128]{2,1,0:T(8,128)S(1)}, u32[]{:S(2)}, u32[]{:S(2)}) collective-permute-start(f32[8,256,128]{2,1,0:T(8,128)S(1)} %get-tuple-element.26), channel_id=1, source_target_pairs={{0,1},{1,2},{2,3},{4,5},{5,6},{6,7},{8,9},{9,10},{10,11},{12,13},{... | collective-permute-start | bytes 3145736 | tf_op jit(solution)/shard_map/ppermute | solution.py:21
  13.4 1.3 collective-permute-start.1
  14.7 7.9 %merge_tiles.6 = (f32[6,256,128]{2,1,0:T(8,128)S(1)}, f32[6,256,256]{2,1,0:T(8,128)S(1)}, f32[6,256,128]{2,1,0:T(8,128)}) custom-call(s32[12]{0:T(128)S(1)} %pad_add_fusion.2.params, bf16[3,32,192,384]{3,2,1,0:T(8,128)(2,1)} %nxt.7, bf16[3,32,192,384]{3,2,1,0:T(8,128)(2,1)} %nxt.7), custom_call_target="tpu_custom_call" | custom-call | flops 3170893824 | bytes 5799936 | tf_op jit(solution)/shard_map/merge_tiles/pallas_call | solution.py:102
  22.6 5.1 %collective-permute-start.10 = (f32[6,256,128]{2,1,0:T(8,128)}, f32[6,256,128]{2,1,0:T(8,128)S(1)}, u32[]{:S(2)}, u32[]{:S(2)}) collective-permute-start(f32[6,256,128]{2,1,0:T(8,128)} %get-tuple-element.35), channel_id=1, source_target_pairs={{0,1},{1,2},{2,3},{4,5},{5,6},{6,7},{8,9},{9,10},{10,11},{12,13},{... | collective-permute-start | bytes 2359304 | tf_op jit(solution)/shard_map/ppermute | solution.py:21
  27.8 1.3 collective-permute-start.11
  29.1 1.6 edge_rows.4
  30.7 11.1 %merge_tiles.5 = (f32[10,256,128]{2,1,0:T(8,128)S(1)}, f32[10,256,256]{2,1,0:T(8,128)S(1)}, f32[10,256,128]{2,1,0:T(8,128)}) custom-call(s32[12]{0:T(128)S(1)} %pad_add_fusion.2.params, bf16[3,32,192,384]{3,2,1,0:T(8,128)(2,1)} %nxt.7, bf16[3,32,192,384]{3,2,1,0:T(8,128)(2,1)} %nxt.7, f32[8,64,256]{2,1,0:T(8,128)S(1)} %get-tuple-element.28.rest_0_), custom_call_target="tpu_custom_call" | custom-call | flops 5284823040 | bytes 9666560 | tf_op jit(solution)/shard_map/merge_tiles/pallas_call | solution.py:102
  41.8 1.5 copy-done
  43.3 5.0 %collective-permute-start.2 = (f32[10,256,128]{2,1,0:T(8,128)}, f32[10,256,128]{2,1,0:T(8,128)S(1)}, u32[]{:S(2)}, u32[]{:S(2)}) collective-permute-start(f32[10,256,128]{2,1,0:T(8,128)} %get-tuple-element.30), channel_id=1, source_target_pairs={{0,1},{1,2},{2,3},{4,5},{5,6},{6,7},{8,9},{9,10},{10,11},{12,13},{... | collective-permute-start | bytes 3932168 | tf_op jit(solution)/shard_map/ppermute | solution.py:21
  48.3 1.3 collective-permute-start.3
  49.8 9.9 %merge_tiles.7 = (f32[8,256,128]{2,1,0:T(8,128)}, f32[8,256,256]{2,1,0:T(8,128)S(1)}, f32[8,256,128]{2,1,0:T(8,128)S(1)}) custom-call(s32[12]{0:T(128)S(1)} %pad_add_fusion.2.params, bf16[3,32,192,384]{3,2,1,0:T(8,128)(2,1)} %nxt.7, bf16[3,32,192,384]{3,2,1,0:T(8,128)(2,1)} %nxt.7, f32[6,64,256]{2,1,0:T(8,128)S(1)} %get-tuple-element.37.rest_0_), custom_call_target="tpu_custom_call" | custom-call | flops 4227858432 | bytes 7733248 | tf_op jit(solution)/shard_map/merge_tiles/pallas_call | solution.py:102
  59.7 3.6 %collective-permute-start.12 = (f32[8,256,128]{2,1,0:T(8,128)S(1)}, f32[8,256,128]{2,1,0:T(8,128)S(1)}, u32[]{:S(2)}, u32[]{:S(2)}) collective-permute-start(f32[8,256,128]{2,1,0:T(8,128)S(1)} %get-tuple-element.39), channel_id=1, source_target_pairs={{0,1},{1,2},{2,3},{4,5},{5,6},{6,7},{8,9},{9,10},{10,11},{12,13},{... | collective-permute-start | bytes 3145736 | tf_op jit(solution)/shard_map/ppermute | solution.py:21
  63.3 1.3 collective-permute-start.13
  64.6 4.2 %collective-permute-start.6 = (s32[3,3]{0,1:T(4,128)S(1)}, s32[3,3]{0,1:T(4,128)S(1)}, u32[]{:S(2)}, u32[]{:S(2)}) collective-permute-start(s32[3,3]{0,1:T(4,128)S(1)} %pad_add_fusion), channel_id=1, source_target_pairs={{0,1},{1,2},{2,3},{4,5},{5,6},{6,7},{8,9},{9,10},{10,11},{12,13},{... | collective-permute-start | bytes 116 | tf_op jit(solution)/shard_map/ppermute | solution.py:21
  68.8 0.8 collective-permute-done.6
  69.6 1.3 collective-permute-start.7
  70.9 8.3 %collective-permute-done.7 = s32[3,3]{0,1:T(4,128)S(1)} collective-permute-done((s32[3,3]{0,1:T(4,128)S(1)}, s32[3,3]{0,1:T(4,128)S(1)}, u32[]{:S(2)}, u32[]{:S(2)}) %collective-permute-start.7) | collective-permute-done | bytes 68 | tf_op jit(solution)/shard_map/ppermute | solution.py:21
  79.3 3.4 %collective-permute-start.8 = (s32[9,3]{0,1:T(4,128)S(1)}, s32[9,3]{0,1:T(4,128)S(1)}, u32[]{:S(2)}, u32[]{:S(2)}) collective-permute-start(s32[9,3]{0,1:T(4,128)S(1)} %pad_add_fusion.1), channel_id=1, source_target_pairs={{0,4},{4,8},{8,12},{12,16},{16,20},{20,24},{24,28},{1,5},{5,9},{9,... | collective-permute-start | bytes 332 | tf_op jit(solution)/shard_map/ppermute | solution.py:21
  82.7 1.3 collective-permute-done.8
  84.0 1.3 collective-permute-start.9
  85.3 4.4 %collective-permute-done.9 = s32[9,3]{0,1:T(4,128)S(1)} collective-permute-done((s32[9,3]{0,1:T(4,128)S(1)}, s32[9,3]{0,1:T(4,128)S(1)}, u32[]{:S(2)}, u32[]{:S(2)}) %collective-permute-start.9) | collective-permute-done | bytes 140 | tf_op jit(solution)/shard_map/ppermute | solution.py:21
  89.7 1.3 collective-permute-start.17
  91.0 1.3 collective-permute-start.19
  92.3 6.1 %collective-permute-start.18 = (f32[6,64,256]{2,1,0:T(8,128)S(1)}, f32[6,64,256]{2,1,0:T(8,128)S(1)}, u32[]{:S(2)}, u32[]{:S(2)}) collective-permute-start(f32[6,64,256]{2,1,0:T(8,128)S(1)} %get-tuple-element.44), channel_id=1, source_target_pairs={{0,4},{4,8},{8,12},{12,16},{16,20},{20,24},{24,28},{1,5},{5,9},{9,... | collective-permute-start | bytes 1179656 | tf_op jit(solution)/shard_map/ppermute | solution.py:21
  98.4 4.3 %edge_rows.5 = (f32[10,64,256]{2,1,0:T(8,128)}, f32[10,64,256]{2,1,0:T(8,128)}) custom-call(f32[10,256,256]{2,1,0:T(8,128)} %copy-done, f32[10,256,128]{2,1,0:T(8,128)S(1)} %collective-permute-done.2.before, f32[10,256,128]{2,1,0:T(8,128)S(1)} %collective-permute-done.3.after), custom_call_target="tpu_custom_call" | custom-call | flops 327680 | bytes 5242880 | tf_op jit(solution)/shard_map/edge_rows/pallas_call | solution.py:152
  102.8 5.7 %collective-permute-start.4 = (f32[10,64,256]{2,1,0:T(8,128)}, f32[10,64,256]{2,1,0:T(8,128)}, u32[]{:S(2)}, u32[]{:S(2)}) collective-permute-start(f32[10,64,256]{2,1,0:T(8,128)} %get-tuple-element.32), channel_id=1, source_target_pairs={{0,4},{4,8},{8,12},{12,16},{16,20},{20,24},{24,28},{1,5},{5,9},{9,... | collective-permute-start | bytes 1966088 | tf_op jit(solution)/shard_map/ppermute | solution.py:21
  108.4 1.3 collective-permute-start.5
  109.7 1.6 edge_rows.7
  111.4 4.3 %collective-permute-done.19.right = f32[6,64,256]{2,1,0:T(8,128)S(1)} collective-permute-done((f32[6,64,256]{2,1,0:T(8,128)S(1)}, f32[6,64,256]{2,1,0:T(8,128)S(1)}, u32[]{:S(2)}, u32[]{:S(2)}) %collective-permute-start.19) | collective-permute-done | bytes 393248 | tf_op jit(solution)/shard_map/ppermute | solution.py:21
  115.6 0.8 copy-done.21
  116.4 5.8 %collective-permute-start.16 = (f32[8,64,256]{2,1,0:T(8,128)}, f32[8,64,256]{2,1,0:T(8,128)}, u32[]{:S(2)}, u32[]{:S(2)}) collective-permute-start(f32[8,64,256]{2,1,0:T(8,128)} %get-tuple-element.43), channel_id=1, source_target_pairs={{0,4},{4,8},{8,12},{12,16},{16,20},{20,24},{24,28},{1,5},{5,9},{9,... | collective-permute-start | bytes 1572872 | tf_op jit(solution)/shard_map/ppermute | solution.py:21
  122.2 16.3 %collective-permute-done.18.left = f32[6,64,256]{2,1,0:T(8,128)S(1)} collective-permute-done((f32[6,64,256]{2,1,0:T(8,128)S(1)}, f32[6,64,256]{2,1,0:T(8,128)S(1)}, u32[]{:S(2)}, u32[]{:S(2)}) %collective-permute-start.18) | collective-permute-done | bytes 393248 | tf_op jit(solution)/shard_map/ppermute | solution.py:21
  139.2 8.7 %collective-permute-start.14 = (f32[8,64,256]{2,1,0:T(8,128)}, f32[8,64,256]{2,1,0:T(8,128)}, u32[]{:S(2)}, u32[]{:S(2)}) collective-permute-start(f32[8,64,256]{2,1,0:T(8,128)} %get-tuple-element.41), channel_id=1, source_target_pairs={{0,4},{4,8},{8,12},{12,16},{16,20},{20,24},{24,28},{1,5},{5,9},{9,... | collective-permute-start | bytes 1572872 | tf_op jit(solution)/shard_map/ppermute | solution.py:21
  147.9 0.8 copy-done.19
  148.7 1.3 collective-permute-start.15
  150.5 1.4 copy-done.4
  151.9 1.1 copy-done.16
  153.1 1.1 copy-done.18
  154.2 1.0 copy-done.22
  155.2 1.0 copy-done.24
  156.2 1.5 finish_slab.4.rest_0_
  157.7 17.4 %collective-permute-done.16.left = f32[8,64,256]{2,1,0:T(8,128)} collective-permute-done((f32[8,64,256]{2,1,0:T(8,128)}, f32[8,64,256]{2,1,0:T(8,128)}, u32[]{:S(2)}, u32[]{:S(2)}) %collective-permute-start.16) | collective-permute-done | bytes 524320 | tf_op jit(solution)/shard_map/ppermute | solution.py:21
  175.1 3.3 %finish_slab.5.rest_0_ = f32[32,128,256]{2,1,0:T(8,128)} custom-call(f32[8,256,256]{2,1,0:T(8,128)S(1)} %get-tuple-element.25.mid, f32[8,256,128]{2,1,0:T(8,128)S(1)} %copy-done.8, f32[8,256,128]{2,1,0:T(8,128)S(1)} %copy-done.10, f32[8,64,256]{2,1,0:T(8,128)} %collective-permute-done.16.left, ...), custom_call_target="tpu_custom_call", output_to_operand_aliasing={{}: (6, {})} | custom-call | flops 1048576 | bytes 5242880 | tf_op jit(solution)/shard_map/finish_slab/pallas_call | solution.py:189
  178.4 7.9 %collective-permute-done.14.left = f32[8,64,256]{2,1,0:T(8,128)} collective-permute-done((f32[8,64,256]{2,1,0:T(8,128)}, f32[8,64,256]{2,1,0:T(8,128)}, u32[]{:S(2)}, u32[]{:S(2)}) %collective-permute-start.14) | collective-permute-done | bytes 524320 | tf_op jit(solution)/shard_map/ppermute | solution.py:21
  186.3 3.5 %finish_slab.6.rest_0_ = f32[32,128,256]{2,1,0:T(8,128)} custom-call(f32[8,256,256]{2,1,0:T(8,128)S(1)} %copy-done.2, f32[8,256,128]{2,1,0:T(8,128)S(1)} %copy-done.12, f32[8,256,128]{2,1,0:T(8,128)S(1)} %copy-done.14, f32[8,64,256]{2,1,0:T(8,128)} %collective-permute-done.14.left, ...), custom_call_target="tpu_custom_call", output_to_operand_aliasing={{}: (6, {})} | custom-call | flops 1048576 | bytes 5242880 | tf_op jit(solution)/shard_map/finish_slab/pallas_call | solution.py:189
  189.8 4.6 %finish_slab.7 = f32[32,128,256]{2,1,0:T(8,128)} custom-call(f32[10,256,256]{2,1,0:T(8,128)} %copy-done, f32[10,256,128]{2,1,0:T(8,128)S(1)} %collective-permute-done.2.before, f32[10,256,128]{2,1,0:T(8,128)S(1)} %copy-done.6, f32[10,64,256]{2,1,0:T(8,128)} %collective-permute-done.4.left, ...), custom_call_target="tpu_custom_call", output_to_operand_aliasing={{}: (6, {})} | custom-call | flops 1310720 | bytes 6553600 | tf_op jit(solution)/shard_map/finish_slab/pallas_call | solution.py:189
  (65 shorter events, 2.3 us)
Async XLA Ops:
  10.9 18.1 %collective-permute-start = (f32[8,256,128]{2,1,0:T(8,128)S(1)}, f32[8,256,128]{2,1,0:T(8,128)S(1)}, u32[]{:S(2)}, u32[]{:S(2)}) collective-permute-start(f32[8,256,128]{2,1,0:T(8,128)S(1)} %get-tuple-element.26), channel_id=1, source_target_pairs={{0,1},{1,2},{2,3},{4,5},{5,6},{6,7},{8,9},{9,10},{10,11},{12,13},{... | collective-permute-start | bytes 3145736 | tf_op jit(solution)/shard_map/ppermute | solution.py:21
  13.4 15.7 %collective-permute-start.1 = (f32[8,256,128]{2,1,0:T(8,128)S(1)}, f32[8,256,128]{2,1,0:T(8,128)S(1)}, u32[]{:S(2)}, u32[]{:S(2)}) collective-permute-start(f32[8,256,128]{2,1,0:T(8,128)S(1)} %get-tuple-element.27), channel_id=1, source_target_pairs={{1,0},{2,1},{3,2},{5,4},{6,5},{7,6},{9,8},{10,9},{11,10},{13,12},{... | collective-permute-start | bytes 3145736 | tf_op jit(solution)/shard_map/ppermute | solution.py:21
  22.6 27.0 %copy-start.3 = (f32[6,256,256]{2,1,0:T(8,128)}, f32[6,256,256]{2,1,0:T(8,128)S(1)}, u32[]{:S(2)}) copy-start(f32[6,256,256]{2,1,0:T(8,128)S(1)} %get-tuple-element.34.mid) | copy-start | bytes 4718596
  22.6 27.0 %collective-permute-start.10 = (f32[6,256,128]{2,1,0:T(8,128)}, f32[6,256,128]{2,1,0:T(8,128)S(1)}, u32[]{:S(2)}, u32[]{:S(2)}) collective-permute-start(f32[6,256,128]{2,1,0:T(8,128)} %get-tuple-element.35), channel_id=1, source_target_pairs={{0,1},{1,2},{2,3},{4,5},{5,6},{6,7},{8,9},{9,10},{10,11},{12,13},{... | collective-permute-start | bytes 2359304 | tf_op jit(solution)/shard_map/ppermute | solution.py:21
  27.8 21.9 %collective-permute-start.11 = (f32[6,256,128]{2,1,0:T(8,128)S(1)}, f32[6,256,128]{2,1,0:T(8,128)S(1)}, u32[]{:S(2)}, u32[]{:S(2)}) collective-permute-start(f32[6,256,128]{2,1,0:T(8,128)S(1)} %get-tuple-element.36), channel_id=1, source_target_pairs={{1,0},{2,1},{3,2},{5,4},{6,5},{7,6},{9,8},{10,9},{11,10},{13,12},{... | collective-permute-start | bytes 2359304 | tf_op jit(solution)/shard_map/ppermute | solution.py:21
  29.1 1.7 copy-start.7
  29.1 1.6 copy-start.9
  41.8 1.5 copy-start
  43.3 47.7 %collective-permute-start.2 = (f32[10,256,128]{2,1,0:T(8,128)}, f32[10,256,128]{2,1,0:T(8,128)S(1)}, u32[]{:S(2)}, u32[]{:S(2)}) collective-permute-start(f32[10,256,128]{2,1,0:T(8,128)} %get-tuple-element.30), channel_id=1, source_target_pairs={{0,1},{1,2},{2,3},{4,5},{5,6},{6,7},{8,9},{9,10},{10,11},{12,13},{... | collective-permute-start | bytes 3932168 | tf_op jit(solution)/shard_map/ppermute | solution.py:21
  48.3 44.0 %collective-permute-start.3 = (f32[10,256,128]{2,1,0:T(8,128)S(1)}, f32[10,256,128]{2,1,0:T(8,128)S(1)}, u32[]{:S(2)}, u32[]{:S(2)}) collective-permute-start(f32[10,256,128]{2,1,0:T(8,128)S(1)} %get-tuple-element.31), channel_id=1, source_target_pairs={{1,0},{2,1},{3,2},{5,4},{6,5},{7,6},{9,8},{10,9},{11,10},{13,12},{... | collective-permute-start | bytes 3932168 | tf_op jit(solution)/shard_map/ppermute | solution.py:21
  49.6 10.1 %copy-start.15 = (f32[6,256,128]{2,1,0:T(8,128)}, f32[6,256,128]{2,1,0:T(8,128)S(1)}, u32[]{:S(2)}) copy-start(f32[6,256,128]{2,1,0:T(8,128)S(1)} %collective-permute-done.10.before) | copy-start | bytes 2359300
  49.6 10.0 %copy-start.17 = (f32[6,256,128]{2,1,0:T(8,128)}, f32[6,256,128]{2,1,0:T(8,128)S(1)}, u32[]{:S(2)}) copy-start(f32[6,256,128]{2,1,0:T(8,128)S(1)} %collective-permute-done.11.after) | copy-start | bytes 2359300
  59.7 50.1 %copy-start.1 = (f32[8,256,256]{2,1,0:T(8,128)}, f32[8,256,256]{2,1,0:T(8,128)S(1)}, u32[]{:S(2)}) copy-start(f32[8,256,256]{2,1,0:T(8,128)S(1)} %get-tuple-element.38.mid) | copy-start | bytes 6291460
  59.7 43.1 %collective-permute-start.12 = (f32[8,256,128]{2,1,0:T(8,128)S(1)}, f32[8,256,128]{2,1,0:T(8,128)S(1)}, u32[]{:S(2)}, u32[]{:S(2)}) collective-permute-start(f32[8,256,128]{2,1,0:T(8,128)S(1)} %get-tuple-element.39), channel_id=1, source_target_pairs={{0,1},{1,2},{2,3},{4,5},{5,6},{6,7},{8,9},{9,10},{10,11},{12,13},{... | collective-permute-start | bytes 3145736 | tf_op jit(solution)/shard_map/ppermute | solution.py:21
  63.3 45.2 %collective-permute-start.13 = (f32[8,256,128]{2,1,0:T(8,128)}, f32[8,256,128]{2,1,0:T(8,128)S(1)}, u32[]{:S(2)}, u32[]{:S(2)}) collective-permute-start(f32[8,256,128]{2,1,0:T(8,128)} %get-tuple-element.40), channel_id=1, source_target_pairs={{1,0},{2,1},{3,2},{5,4},{6,5},{7,6},{9,8},{10,9},{11,10},{13,12},{... | collective-permute-start | bytes 3145736 | tf_op jit(solution)/shard_map/ppermute | solution.py:21
  64.6 5.0 %collective-permute-start.6 = (s32[3,3]{0,1:T(4,128)S(1)}, s32[3,3]{0,1:T(4,128)S(1)}, u32[]{:S(2)}, u32[]{:S(2)}) collective-permute-start(s32[3,3]{0,1:T(4,128)S(1)} %pad_add_fusion), channel_id=1, source_target_pairs={{0,1},{1,2},{2,3},{4,5},{5,6},{6,7},{8,9},{9,10},{10,11},{12,13},{... | collective-permute-start | bytes 116 | tf_op jit(solution)/shard_map/ppermute | solution.py:21
  69.6 9.6 %collective-permute-start.7 = (s32[3,3]{0,1:T(4,128)S(1)}, s32[3,3]{0,1:T(4,128)S(1)}, u32[]{:S(2)}, u32[]{:S(2)}) collective-permute-start(s32[3,3]{0,1:T(4,128)S(1)} %pad_add_fusion), channel_id=1, source_target_pairs={{1,0},{2,1},{3,2},{5,4},{6,5},{7,6},{9,8},{10,9},{11,10},{13,12},{... | collective-permute-start | bytes 116 | tf_op jit(solution)/shard_map/ppermute | solution.py:21
  79.3 4.7 %collective-permute-start.8 = (s32[9,3]{0,1:T(4,128)S(1)}, s32[9,3]{0,1:T(4,128)S(1)}, u32[]{:S(2)}, u32[]{:S(2)}) collective-permute-start(s32[9,3]{0,1:T(4,128)S(1)} %pad_add_fusion.1), channel_id=1, source_target_pairs={{0,4},{4,8},{8,12},{12,16},{16,20},{20,24},{24,28},{1,5},{5,9},{9,... | collective-permute-start | bytes 332 | tf_op jit(solution)/shard_map/ppermute | solution.py:21
  84.0 5.7 %collective-permute-start.9 = (s32[9,3]{0,1:T(4,128)S(1)}, s32[9,3]{0,1:T(4,128)S(1)}, u32[]{:S(2)}, u32[]{:S(2)}) collective-permute-start(s32[9,3]{0,1:T(4,128)S(1)} %pad_add_fusion.1), channel_id=1, source_target_pairs={{4,0},{8,4},{12,8},{16,12},{20,16},{24,20},{28,24},{5,1},{9,5},{13... | collective-permute-start | bytes 332 | tf_op jit(solution)/shard_map/ppermute | solution.py:21
  89.7 58.2 %collective-permute-start.17 = (f32[8,64,256]{2,1,0:T(8,128)S(1)}, f32[8,64,256]{2,1,0:T(8,128)S(1)}, u32[]{:S(2)}, u32[]{:S(2)}) collective-permute-start(f32[8,64,256]{2,1,0:T(8,128)S(1)} %get-tuple-element.28.rest_0_), channel_id=1, source_target_pairs={{4,0},{8,4},{12,8},{16,12},{20,16},{24,20},{28,24},{5,1},{9,5},{13... | collective-permute-start | bytes 1572872 | tf_op jit(solution)/shard_map/ppermute | solution.py:21
  91.0 24.6 %collective-permute-start.19 = (f32[6,64,256]{2,1,0:T(8,128)S(1)}, f32[6,64,256]{2,1,0:T(8,128)S(1)}, u32[]{:S(2)}, u32[]{:S(2)}) collective-permute-start(f32[6,64,256]{2,1,0:T(8,128)S(1)} %get-tuple-element.37.rest_0_), channel_id=1, source_target_pairs={{4,0},{8,4},{12,8},{16,12},{20,16},{24,20},{28,24},{5,1},{9,5},{13... | collective-permute-start | bytes 1179656 | tf_op jit(solution)/shard_map/ppermute | solution.py:21
  92.3 10.4 %copy-start.5 = (f32[10,256,128]{2,1,0:T(8,128)}, f32[10,256,128]{2,1,0:T(8,128)S(1)}, u32[]{:S(2)}) copy-start(f32[10,256,128]{2,1,0:T(8,128)S(1)} %collective-permute-done.3.after) | copy-start | bytes 3932164
  92.3 46.1 %collective-permute-start.18 = (f32[6,64,256]{2,1,0:T(8,128)S(1)}, f32[6,64,256]{2,1,0:T(8,128)S(1)}, u32[]{:S(2)}, u32[]{:S(2)}) collective-permute-start(f32[6,64,256]{2,1,0:T(8,128)S(1)} %get-tuple-element.44), channel_id=1, source_target_pairs={{0,4},{4,8},{8,12},{12,16},{16,20},{20,24},{24,28},{1,5},{5,9},{9,... | collective-permute-start | bytes 1179656 | tf_op jit(solution)/shard_map/ppermute | solution.py:21
  102.8 8.6 %copy-start.11 = (f32[8,256,128]{2,1,0:T(8,128)}, f32[8,256,128]{2,1,0:T(8,128)S(1)}, u32[]{:S(2)}) copy-start(f32[8,256,128]{2,1,0:T(8,128)S(1)} %collective-permute-done.12.before) | copy-start | bytes 3145732
  102.8 87.0 %collective-permute-start.4 = (f32[10,64,256]{2,1,0:T(8,128)}, f32[10,64,256]{2,1,0:T(8,128)}, u32[]{:S(2)}, u32[]{:S(2)}) collective-permute-start(f32[10,64,256]{2,1,0:T(8,128)} %get-tuple-element.32), channel_id=1, source_target_pairs={{0,4},{4,8},{8,12},{12,16},{16,20},{20,24},{24,28},{1,5},{5,9},{9,... | collective-permute-start | bytes 1966088 | tf_op jit(solution)/shard_map/ppermute | solution.py:21
  108.4 2.9 %copy-start.13 = (f32[8,256,128]{2,1,0:T(8,128)}, f32[8,256,128]{2,1,0:T(8,128)S(1)}, u32[]{:S(2)}) copy-start(f32[8,256,128]{2,1,0:T(8,128)S(1)} %collective-permute-done.13.after) | copy-start | bytes 3145732
  108.4 81.4 %collective-permute-start.5 = (f32[10,64,256]{2,1,0:T(8,128)}, f32[10,64,256]{2,1,0:T(8,128)}, u32[]{:S(2)}, u32[]{:S(2)}) collective-permute-start(f32[10,64,256]{2,1,0:T(8,128)} %get-tuple-element.33), channel_id=1, source_target_pairs={{4,0},{8,4},{12,8},{16,12},{20,16},{24,20},{28,24},{5,1},{9,5},{13... | collective-permute-start | bytes 1966088 | tf_op jit(solution)/shard_map/ppermute | solution.py:21
  115.6 0.8 copy-start.21
  116.4 58.7 %collective-permute-start.16 = (f32[8,64,256]{2,1,0:T(8,128)}, f32[8,64,256]{2,1,0:T(8,128)}, u32[]{:S(2)}, u32[]{:S(2)}) collective-permute-start(f32[8,64,256]{2,1,0:T(8,128)} %get-tuple-element.43), channel_id=1, source_target_pairs={{0,4},{4,8},{8,12},{12,16},{16,20},{20,24},{24,28},{1,5},{5,9},{9,... | collective-permute-start | bytes 1572872 | tf_op jit(solution)/shard_map/ppermute | solution.py:21
  138.5 0.8 copy-start.23
  139.2 47.1 %collective-permute-start.14 = (f32[8,64,256]{2,1,0:T(8,128)}, f32[8,64,256]{2,1,0:T(8,128)}, u32[]{:S(2)}, u32[]{:S(2)}) collective-permute-start(f32[8,64,256]{2,1,0:T(8,128)} %get-tuple-element.41), channel_id=1, source_target_pairs={{0,4},{4,8},{8,12},{12,16},{16,20},{20,24},{24,28},{1,5},{5,9},{9,... | collective-permute-start | bytes 1572872 | tf_op jit(solution)/shard_map/ppermute | solution.py:21
  147.9 0.8 copy-start.19
  148.7 37.6 %collective-permute-start.15 = (f32[8,64,256]{2,1,0:T(8,128)}, f32[8,64,256]{2,1,0:T(8,128)}, u32[]{:S(2)}, u32[]{:S(2)}) collective-permute-start(f32[8,64,256]{2,1,0:T(8,128)} %get-tuple-element.42), channel_id=1, source_target_pairs={{4,0},{8,4},{12,8},{16,12},{20,16},{24,20},{28,24},{5,1},{9,5},{13... | collective-permute-start | bytes 1572872 | tf_op jit(solution)/shard_map/ppermute | solution.py:21
  150.5 1.4 copy-start.4
  151.9 1.1 copy-start.16
  153.0 1.1 copy-start.18
  154.2 1.0 copy-start.22
  155.2 1.0 copy-start.24
  156.2 18.9 %copy-start.8 = (f32[8,256,128]{2,1,0:T(8,128)S(1)}, f32[8,256,128]{2,1,0:T(8,128)}, u32[]{:S(2)}) copy-start(f32[8,256,128]{2,1,0:T(8,128)} %copy-done.7) | copy-start | bytes 3145732
  156.2 18.9 %copy-start.10 = (f32[8,256,128]{2,1,0:T(8,128)S(1)}, f32[8,256,128]{2,1,0:T(8,128)}, u32[]{:S(2)}) copy-start(f32[8,256,128]{2,1,0:T(8,128)} %copy-done.9) | copy-start | bytes 3145732
  156.2 18.9 %copy-start.20 = (f32[8,64,256]{2,1,0:T(8,128)S(1)}, f32[8,64,256]{2,1,0:T(8,128)}, u32[]{:S(2)}) copy-start(f32[8,64,256]{2,1,0:T(8,128)} %copy-done.19) | copy-start | bytes 1572868
  157.7 28.6 %copy-start.2 = (f32[8,256,256]{2,1,0:T(8,128)S(1)}, f32[8,256,256]{2,1,0:T(8,128)}, u32[]{:S(2)}) copy-start(f32[8,256,256]{2,1,0:T(8,128)} %copy-done.1) | copy-start | bytes 6291460
  157.7 28.6 %copy-start.12 = (f32[8,256,128]{2,1,0:T(8,128)S(1)}, f32[8,256,128]{2,1,0:T(8,128)}, u32[]{:S(2)}) copy-start(f32[8,256,128]{2,1,0:T(8,128)} %copy-done.11) | copy-start | bytes 3145732
  157.7 28.6 %copy-start.14 = (f32[8,256,128]{2,1,0:T(8,128)S(1)}, f32[8,256,128]{2,1,0:T(8,128)}, u32[]{:S(2)}) copy-start(f32[8,256,128]{2,1,0:T(8,128)} %copy-done.13) | copy-start | bytes 3145732
  178.4 11.4 %copy-start.6 = (f32[10,256,128]{2,1,0:T(8,128)S(1)}, f32[10,256,128]{2,1,0:T(8,128)}, u32[]{:S(2)}) copy-start(f32[10,256,128]{2,1,0:T(8,128)} %copy-done.5) | copy-start | bytes 3932164
